TPU v7x, 256 devices: a 4x2x16 block of a 4x16x16 slice. The times are simulated.
256 devices in a mesh: groups: 2 (over y), seq: 8 (over x, core), tensor: 16 (over z).
Axes of the slice: x: 4, y: 2, z: 16, core: 2. Of those that a mesh axis runs over, the one named last changes fastest.
The devices are a block of a 4x16x16 slice.
Arguments:
- hidden: bfloat16 [512, 4608], P(('groups', 'seq')), parts along dimension 0, may hold values from -6 to 6
- pre_gain: float32 [4608], replicated, may hold values from 0.25 to 1.75
- w_query: bfloat16 [4608, 4096], P(None, 'tensor'), may hold values from -0.09375 to 0.09375
- w_key: bfloat16 [4608, 2048], P(None, 'tensor'), may hold values from -0.09375 to 0.09375
- w_value: bfloat16 [4608, 2048], P(None, 'tensor'), may hold values from -0.09375 to 0.09375
- w_out: bfloat16 [4096, 4608], P('tensor'), may hold values from -0.125 to 0.125
- post_gain: float32 [4608], P('tensor'), may hold values from 0.25 to 1.75
- cache_pool: bfloat16 [1024, 2, 128, 2048], P(('groups', 'seq'), None, None, 'tensor'), parts along dimension 0, may hold values from -6 to 6
- prompt_cache: bfloat16 [256, 2, 64, 2048], P('seq', None, None, 'tensor'), may hold values from -6 to 6
- task_ids: int32 [512], P('groups'), parts along dimension 0, may hold values from 0 to 255
- cache_lengths: int32 [512], P('groups'), parts along dimension 0, may hold values from 1 to 4096, as said below
- block_table: int32 [512, 32], P('groups'), parts along dimension 0, may hold values from -1 to 511, as said below
Outputs:
- layer_out: bfloat16 [512, 4608], P(('groups', 'seq'), 'tensor'), parts along dimension 0
- fresh_cache: bfloat16 [512, 2, 2048], P(('groups', 'seq'), None, 'tensor'), parts along dimension 0
There are 2 independent parts, one for each index of `groups`. A program takes and returns all parts, laid end to end along the dimension named above; an argument that names none is the same for every part. Nothing has to cross between parts.
Inputs may be any that keep to these rules, and one draw needn't show every extreme that they name: `cache_lengths`: each draw has a request with exactly 4096 cache tokens. block_table[r, j] is the page of cache_pool holding cache tokens j * 128 to (j + 1) * 128 - 1 of request r for j < ceil(cache_lengths[r] / 128), and -1 for the later j; no page is named twice.
All inputs are finite; a program needn't handle non-finite values.
Results may differ from a plain program's by a relative error of at most 0.018.
Values may be sent and summed in bfloat16 or wider, within the bound.
A program may use at most 64 MiB of HBM per device.

v0:
```python
import jax
import jax.numpy as jnp
from jax import lax
from jax.sharding import PartitionSpec as P

D = 4608
H = 32
HD = 128


cap_limit = 50.0


def from_everyone(x, axis):
    size = lax.axis_size(axis)
    return lax.all_to_all(jnp.broadcast_to(x[None], (size, *x.shape)), axis, 0, 0, tiled=True)


def in_order(tiles, dim):
    lengths = list(tiles.shape[1:])
    lengths[dim] *= tiles.shape[0]
    return jnp.moveaxis(tiles, 0, dim).reshape(lengths)


def gather_directly(x, axis, dim):
    tiles = from_everyone(x, axis)
    return in_order(tiles, dim)


def in_blocks(x, dim, size):
    before, after = (x.shape[:dim], x.shape[dim + 1 :])
    return jnp.moveaxis(x.reshape(*before, size, -1, *after), dim, 0)


def sent_and_summed(x, axis, dim):
    size = lax.axis_size(axis)
    tiles = lax.all_to_all(in_blocks(x, dim, size), axis, 0, 0, tiled=True)
    return jnp.sum(tiles.astype(jnp.float32), axis=0)


def in_one_piece(arrays, axis, dim, along):
    both = jnp.concatenate(arrays, axis=along)
    whole, at, finished = (sent_and_summed(both, axis, dim), 0, [])
    for a in arrays:
        finished.append(lax.slice_in_dim(whole, at, at + a.shape[along], axis=along))
        at += a.shape[along]
    return tuple(finished)


def of_everyone(x, axis):
    everything = from_everyone(x, axis)
    return jnp.sum(everything, axis=0)


def rms_scale(values, gain):
    mean_square = jnp.mean(values * values, axis=-1, keepdims=True)
    return values * lax.rsqrt(mean_square + 1e-06) * gain


def rotate(values, position):
    half_dim = values.shape[-1] // 2
    frequency = 10000.0 ** (-jnp.arange(half_dim, dtype=jnp.float32) / half_dim)
    angles = position.astype(jnp.float32)[:, None] * frequency[None, :]
    cosine = jnp.cos(angles)[:, None, :]
    sines = jnp.sin(angles)[:, None, :]
    first_half = values[..., :half_dim]
    second_half = values[..., half_dim:]
    return jnp.concatenate(
        [first_half * cosine - second_half * sines, second_half * cosine + first_half * sines],
        axis=-1,
    )


def capped(raw_score, score_scale):
    return cap_limit * jnp.tanh(raw_score * score_scale / cap_limit)


def attend(query_block, block, live_mask, score_scale):
    count = block.shape[0]
    length = block.shape[2]
    kv_heads = query_block.shape[1]
    head_dim = query_block.shape[3]
    block_keys = block[:, 0].reshape(count, length, kv_heads, head_dim)
    block_values = block[:, 1].reshape(count, length, kv_heads, head_dim)
    raw_score = jnp.einsum(
        "nkgd,ntkd->nkgt", query_block, block_keys, preferred_element_type=jnp.float32
    )
    weight = jnp.where(live_mask[:, None, None, :], jnp.exp(capped(raw_score, score_scale)), 0.0)
    totals = jnp.sum(weight, axis=-1).reshape(count, -1)
    mixtures = jnp.einsum(
        "nkgt,ntkd->nkgd",
        weight.astype(jnp.bfloat16),
        block_values,
        preferred_element_type=jnp.float32,
    )
    return (totals, mixtures.reshape(count, -1))


def body(
    hidden,
    pre_gain,
    w_query,
    w_key,
    w_value,
    w_out,
    post_gain,
    cache_pool,
    prompt_cache,
    task_ids,
    cache_lengths,
    block_table,
):
    seq_index = lax.axis_index("seq")
    tensor_index = lax.axis_index("tensor")
    own_rows = hidden.shape[0]
    requests = task_ids.shape[0]
    pages_dev = cache_pool.shape[0]
    block_len = cache_pool.shape[2]
    kv_width = cache_pool.shape[3]
    head_dim = HD
    kv_heads = kv_width // head_dim
    query_heads = w_query.shape[1] // head_dim
    group_size = query_heads // kv_heads
    prompt_len = prompt_cache.shape[2]
    tasks_dev = prompt_cache.shape[0]
    score_scale = float(D // H) ** (-0.5)
    first_row = seq_index * own_rows
    own_lengths = lax.dynamic_slice_in_dim(cache_lengths, first_row, own_rows)
    normed = rms_scale(hidden.astype(jnp.float32), pre_gain).astype(jnp.bfloat16)
    position = prompt_len + own_lengths
    query_rows = rotate(
        jnp.dot(normed, w_query, preferred_element_type=jnp.float32).reshape(
            own_rows, query_heads, head_dim
        ),
        position,
    ).astype(jnp.bfloat16)
    key_new = rotate(
        jnp.dot(normed, w_key, preferred_element_type=jnp.float32).reshape(
            own_rows, kv_heads, head_dim
        ),
        position,
    ).astype(jnp.bfloat16)
    value_new = jnp.dot(normed, w_value, preferred_element_type=jnp.float32).astype(jnp.bfloat16)
    fresh_cache = jnp.stack([key_new.reshape(own_rows, kv_width), value_new], axis=1)
    queries = gather_directly(query_rows.reshape(own_rows, query_heads * head_dim), "seq", 0)
    page_ids = seq_index * pages_dev + jnp.arange(pages_dev)
    flat_table = block_table.reshape(-1)
    max_blocks = block_table.shape[1]
    matches = flat_table[None, :] == page_ids[:, None]
    entry_index = jnp.arange(flat_table.shape[0])
    page_used = jnp.any(matches, axis=1)
    found_entry = jnp.sum(jnp.where(matches, entry_index[None, :], 0), axis=1)
    page_owner = found_entry // max_blocks
    block_number = found_entry % max_blocks
    owner_hot = (page_owner[:, None] == jnp.arange(requests)[None, :]) & page_used[:, None]
    owner_length = jnp.sum(jnp.where(owner_hot, cache_lengths[None, :], 0), axis=1)
    valid_count = jnp.clip(owner_length - block_number * block_len, 0, block_len)
    page_query = jnp.dot(
        owner_hot.astype(jnp.bfloat16), queries, preferred_element_type=jnp.float32
    ).astype(jnp.bfloat16)
    page_query = page_query.reshape(pages_dev, kv_heads, group_size, head_dim)
    page_live = jnp.arange(block_len)[None, :] < valid_count[:, None]
    page_totals, page_mixtures = attend(page_query, cache_pool, page_live, score_scale)
    spread_hot = owner_hot.astype(jnp.float32).T
    totals = jnp.dot(spread_hot, page_totals)
    mixtures = jnp.dot(spread_hot, page_mixtures)
    local_task = task_ids - seq_index * tasks_dev
    is_owned = (local_task >= 0) & (local_task < tasks_dev)
    task_rows = prompt_cache[jnp.clip(local_task, 0, tasks_dev - 1)]
    all_query = queries.reshape(requests, kv_heads, group_size, head_dim)
    owned_live = jnp.broadcast_to(is_owned[:, None], (requests, prompt_len))
    prompt_totals, prompt_mixtures = attend(all_query, task_rows, owned_live, score_scale)
    totals = totals + prompt_totals
    mixtures = mixtures + prompt_mixtures
    totals, mixtures = in_one_piece(
        (totals.astype(jnp.bfloat16), mixtures.astype(jnp.bfloat16)), "seq", 0, 1
    )
    own_query = query_rows.reshape(own_rows, kv_heads, group_size, head_dim)
    self_raw = jnp.sum(
        own_query.astype(jnp.float32) * key_new[:, :, None, :].astype(jnp.float32), axis=-1
    )
    self_weight = jnp.exp(capped(self_raw, score_scale))
    rounded = lax.optimization_barrier(self_weight.astype(jnp.bfloat16)).astype(jnp.float32)
    totals = totals + self_weight.reshape(own_rows, -1)
    self_mix = rounded[..., None] * value_new.reshape(own_rows, kv_heads, 1, head_dim).astype(
        jnp.float32
    )
    mixtures = mixtures + self_mix.reshape(own_rows, -1)
    attended = (mixtures.reshape(own_rows, query_heads, head_dim) / totals[..., None]).astype(
        jnp.bfloat16
    )
    projected = jnp.dot(
        attended.reshape(own_rows, query_heads * head_dim),
        w_out,
        preferred_element_type=jnp.float32,
    )
    cols_local = post_gain.shape[0]
    col_start = tensor_index * cols_local
    residual = lax.dynamic_slice_in_dim(hidden, col_start, cols_local, 1).astype(jnp.float32)
    share_cols = sent_and_summed(projected.astype(jnp.bfloat16), "tensor", 1)
    squares = of_everyone(jnp.sum(share_cols * share_cols, axis=1), "tensor")
    scaled = share_cols * lax.rsqrt(squares[:, None] / D + 1e-06)
    layer_out = (residual + scaled * post_gain).astype(jnp.bfloat16)
    return (layer_out, fresh_cache)


def solution(mesh):
    return jax.shard_map(
        body,
        mesh=mesh,
        in_specs=(
            P(("groups", "seq"), None),
            P(),
            P(None, "tensor"),
            P(None, "tensor"),
            P(None, "tensor"),
            P("tensor", None),
            P("tensor"),
            P(("groups", "seq"), None, None, "tensor"),
            P("seq", None, None, "tensor"),
            P("groups"),
            P("groups"),
            P("groups", None),
        ),
        out_specs=(P(("groups", "seq"), "tensor"), P(("groups", "seq"), None, "tensor")),
        check_vma=False,
    )
```

profile of v0, /device:TPU:40, one launch (start us, length us, event | category | flops | bytes accessed | tf_op | source)
XLA Modules:
  0.0 129.3 jit_solution(15988120681580040520)
XLA Ops:
  0.7 1.3 fusion.31
  2.0 0.5 copy-done.4
  2.5 2.3 %fusion.64 = f32[32,256]{1,0:T(8,128)S(1)} fusion(bf16[4608,256]{1,0:T(8,128)(2,1)} %param.14, bf16[32,4608]{1,0:T(8,128)(2,1)} %param.12, f32[4608]{0:T(1024)} %param.13, f32[32]{0:T(128)S(1)} %add_rsqrt_fusion.1), kind=kOutput, calls=%fused_computation.100 | convolution fusion | flops 76087296 | bytes 2705536 | tf_op jit(solution)/shard_map/dot_general | solution.py:132
  5.0 0.1 multiply_cosine_fusion.1
  5.1 0.4 copy-done.8
  5.5 0.1 subtract_convert_fusion
  5.7 0.1 pad_maximum_fusion.1
  5.8 0.6 broadcast_in_dim.59
  6.4 4.6 %all-to-all-start = ((bf16[8,32,256]{2,1,0:T(8,128)(2,1)}), bf16[8,32,256]{2,1,0:T(8,128)(2,1)}, u32[]{:S(2)}, u32[]{:S(2)}) async-start(bf16[8,32,256]{2,1,0:T(8,128)(2,1)} %broadcast_in_dim.59), calls=%async_computation | async-start | bytes 262144 | tf_op jit(solution)/shard_map/all_to_all | solution.py:16
  11.0 0.5 iota_add_fusion
  11.6 0.9 copy.65
  12.4 0.7 eq.30
  13.1 1.1 fusion.2
  14.3 1.2 compare_reduce_fusion
  15.5 0.7 compare_select_fusion.1
  16.2 1.2 compare_and_fusion
  17.4 0.9 select_reduce_fusion
  18.4 1.7 %convolution_bitcast_fusion = f32[32,1,128]{2,0,1:T(8,128)S(1)} fusion(bf16[4608,128]{1,0:T(8,128)(2,1)} %param.15, bf16[32,4608]{1,0:T(8,128)(2,1)} %param.12, f32[4608]{0:T(1024)} %param.13, f32[32]{0:T(128)} %copy-done.4), kind=kOutput, calls=%fused_computation.27 | convolution fusion | flops 38338560 | bytes 1509504 | tf_op jit(solution)/shard_map/dot_general | solution.py:138
  20.1 0.8 fusion.54
  20.9 1.7 %fusion.68 = (f32[32,128]{1,0:T(8,128)S(1)}, bf16[32,128]{1,0:T(8,128)(2,1)S(1)}) fusion(bf16[4608,128]{1,0:T(8,128)(2,1)} %param.16, bf16[32,4608]{1,0:T(8,128)(2,1)} %param.12, f32[4608]{0:T(1024)} %param.13, f32[32]{0:T(128)} %copy-done.4), kind=kOutput, calls=%fused_computation.103 | convolution fusion | flops 38346752 | bytes 1517696 | tf_op jit(solution)/shard_map/dot_general | solution.py:143
  22.7 8.4 %gather_fusion = bf16[256,2,64,128]{3,2,1,0:T(8,128)(2,1)} fusion(bf16[32,2,64,128]{3,2,1,0:T(8,128)(2,1)S(1)} %copy-done.1, s32[1024]{0:T(1024)S(1)} %pad_clamp_fusion), kind=kCustom, calls=%fused_computation | custom fusion | bytes 16778240 | tf_op jit(solution)/shard_map/gather | solution.py:169
  31.2 1.1 convolution_convert_fusion.1
  32.3 0.9 reshape.423
  33.3 4.6 %fusion.66 = (f32[256,2]{1,0:T(8,128)S(1)}, bf16[256,2,64]{2,1,0:T(2,128)(2,1)S(1)}) fusion(bf16[256,2,128]{2,1,0:T(2,128)(2,1)S(1)} %reshape.423, bf16[256,2,64,128]{3,2,1,0:T(8,128)(2,1)} %gather_fusion, pred[256]{0:T(512)(128)(4,1)} %compare_and_fusion), kind=kOutput, calls=%fused_computation.101 | convolution fusion | flops 8551936 | bytes 4393472 | tf_op jit(solution)/shard_map/nkgd,ntkd->nkgt/dot_general | solution.py:85
  37.9 0.1 copy.68
  38.0 2.9 %fusion.67 = (bf16[64,2]{1,0:T(8,128)(2,1)S(1)}, bf16[64,2,128]{2,1,0:T(2,128)(2,1)S(1)}) fusion(bf16[64,2,128]{2,1,0:T(2,128)(2,1)S(1)} %reshape.421, bf16[64,2,128,128]{3,2,1,0:T(8,128)(2,1)} %param.19, pred[64,128]{1,0:T(8,128)(4,1)S(1)} %iota_compare_fusion.1), kind=kOutput, calls=%fused_computation.102 | convolution fusion | flops 4276096 | bytes 2171136 | tf_op jit(solution)/shard_map/nkgd,ntkd->nkgt/dot_general | solution.py:85
  40.9 2.3 %fusion.3 = bf16[64,2,128]{2,1,0:T(2,128)(2,1)S(1)} fusion(bf16[64,2,128,128]{3,2,1,0:T(8,128)(2,1)} %param.19, bf16[64,2,128]{2,1,0:T(2,128)(2,1)S(1)} %get-tuple-element.25), kind=kOutput, calls=%fused_computation.9 | convolution fusion | flops 4194304 | bytes 2162688 | tf_op jit(solution)/shard_map/nkgt,ntkd->nkgd/dot_general | solution.py:90
  43.1 3.4 %fusion = f32[256,2,128]{2,1,0:T(2,128)S(1)} fusion(bf16[256,2,64,128]{3,2,1,0:T(8,128)(2,1)} %gather_fusion, bf16[256,2,64]{2,1,0:T(2,128)(2,1)S(1)} %get-tuple-element.23), kind=kOutput, calls=%fused_computation.3 | convolution fusion | flops 8388608 | bytes 4521984 | tf_op jit(solution)/shard_map/nkgt,ntkd->nkgd/dot_general | solution.py:90
  46.6 0.2 copy.71
  46.7 0.2 fusion.29
  47.0 0.3 fusion.11
  47.3 0.8 copy.72
  48.1 4.9 %all-to-all-start.1 = ((bf16[8,32,258]{2,1,0:T(8,128)(2,1)}), bf16[8,32,258]{2,1,0:T(8,128)(2,1)S(1)}, u32[]{:S(2)}, u32[]{:S(2)}) async-start(bf16[8,32,258]{2,1,0:T(8,128)(2,1)} %bitcast.6), calls=%async_computation.1 | async-start | bytes 393216 | tf_op jit(solution)/shard_map/all_to_all | solution.py:37
  53.0 0.2 multiply_reduce_fusion.1
  53.2 6.5 %all-to-all-done.1 = bf16[8,32,258]{2,1,0:T(8,128)(2,1)S(1)} async-done(((bf16[8,32,258]{2,1,0:T(8,128)(2,1)}), bf16[8,32,258]{2,1,0:T(8,128)(2,1)S(1)}, u32[]{:S(2)}, u32[]{:S(2)}) %all-to-all-start.1) | async-done | bytes 132128 | tf_op jit(solution)/shard_map/all_to_all | solution.py:37
  59.9 0.1 copy.74
  60.0 0.1 copy.76
  60.1 0.1 broadcast_multiply_fusion
  60.2 0.1 div.62
  60.3 0.5 convolution_convert_fusion
  60.9 0.6 reshape.431
  61.5 46.7 %all_to_all.21 = bf16[16,32,288]{2,1,0:T(8,128)(2,1)S(1)} all-to-all(bf16[16,32,288]{2,1,0:T(8,128)(2,1)S(1)} %bitcast.93), channel_id=1, replica_groups=mesh['groups'=2,'seq'=8,'tensor'=16] {'tensor'}, dimensions={0} | all-to-all | bytes 589824 | tf_op jit(solution)/shard_map/all_to_all | solution.py:37
  108.3 0.1 multiply_reduce_fusion
  108.5 0.6 broadcast_in_dim.64
  109.1 6.5 %all-to-all-start.3 = ((f32[16,1,32]{2,1,0:T(1,128)}), f32[16,1,32]{2,1,0:T(1,128)S(1)}, u32[]{:S(2)}, u32[]{:S(2)}) async-start(f32[16,1,32]{2,1,0:T(1,128)} %broadcast_in_dim.64), calls=%async_computation.3 | async-start | bytes 16384 | tf_op jit(solution)/shard_map/all_to_all | solution.py:16
  115.7 0.6 copy.79
  116.3 11.5 %all-to-all-done.3 = f32[16,1,32]{2,1,0:T(1,128)S(1)} async-done(((f32[16,1,32]{2,1,0:T(1,128)}), f32[16,1,32]{2,1,0:T(1,128)S(1)}, u32[]{:S(2)}, u32[]{:S(2)}) %all-to-all-start.3) | async-done | bytes 2080 | tf_op jit(solution)/shard_map/all_to_all | solution.py:16
  127.8 1.5 %add_convert_fusion = bf16[32,288]{1,0:T(8,128)(2,1)} fusion(f32[32,288]{1,0:T(8,128)S(1)} %convert_reduce_fusion, f32[288]{0:T(512)S(1)} %copy-done.11, f32[32]{0:T(128)S(1)} %add_rsqrt_fusion, bf16[32,4608]{1,0:T(8,128)(2,1)} %param.12, s32[]{:T(128)S(6)} %select_n.47), kind=kLoop, calls=%fused_computation.47 | loop fusion | flops 46080 | bytes 75012 | tf_op jit(solution)/shard_map/convert_element_type | solution.py:203
  (48 shorter events, 0.9 us)
Async XLA Ops:
  0.6 59.7 %copy-start = (bf16[256,4608]{1,0:T(8,128)(2,1)S(1)}, bf16[256,4608]{1,0:T(8,128)(2,1)}, u32[]{:S(2)}) copy-start(bf16[256,4608]{1,0:T(8,128)(2,1)} %param.17) | copy-start | bytes 7077892
  0.6 4.2 %copy-start.12 = (s32[256]{0:T(256)S(1)}, s32[256]{0:T(256)}, u32[]{:S(2)}) copy-start(s32[256]{0:T(256)} %param.22) | copy-start | bytes 3076
  0.7 10.3 %copy-start.7 = (f32[64]{0:T(128)}, f32[64]{0:T(128)S(1)}, u32[]{:S(2)}) copy-start(f32[64]{0:T(128)S(1)} %multiply_power_fusion) | copy-start | bytes 772
  2.0 0.5 copy-start.4
  4.8 17.9 %copy-start.1 = (bf16[32,2,64,128]{3,2,1,0:T(8,128)(2,1)S(1)}, bf16[32,2,64,128]{3,2,1,0:T(8,128)(2,1)}, u32[]{:S(2)}) copy-start(bf16[32,2,64,128]{3,2,1,0:T(8,128)(2,1)} %param.20) | copy-start | bytes 3145732
  5.0 0.6 copy-start.8
  5.7 5.4 %copy-start.2 = (bf16[32,2,64]{2,1,0:T(2,128)(2,1)}, bf16[32,2,64]{2,1,0:T(2,128)(2,1)S(1)}, u32[]{:S(2)}) copy-start(bf16[32,2,64]{2,1,0:T(2,128)(2,1)S(1)} %get-tuple-element.15) | copy-start | bytes 24580
  6.4 24.8 %all-to-all-start = ((bf16[8,32,256]{2,1,0:T(8,128)(2,1)}), bf16[8,32,256]{2,1,0:T(8,128)(2,1)}, u32[]{:S(2)}, u32[]{:S(2)}) async-start(bf16[8,32,256]{2,1,0:T(8,128)(2,1)} %broadcast_in_dim.59), calls=%async_computation | async-start | bytes 262144 | tf_op jit(solution)/shard_map/all_to_all | solution.py:16
  15.5 15.7 %copy-start.5 = (pred[64]{0:T(512)(128)(4,1)}, pred[64]{0:T(512)(128)(4,1)S(1)}, u32[]{:S(2)}) copy-start(pred[64]{0:T(512)(128)(4,1)S(1)} %compare_reduce_fusion) | copy-start | bytes 196
  17.4 13.8 %copy-start.9 = (s32[64]{0:T(128)}, s32[64]{0:T(128)S(1)}, u32[]{:S(2)}) copy-start(s32[64]{0:T(128)S(1)} %and_select_fusion.1) | copy-start | bytes 772
  43.1 3.6 %copy-start.6 = (pred[64]{0:T(512)(128)(4,1)S(1)}, pred[64]{0:T(512)(128)(4,1)}, u32[]{:S(2)}) copy-start(pred[64]{0:T(512)(128)(4,1)} %copy-done.5) | copy-start | bytes 196
  43.1 3.6 %copy-start.10 = (s32[64]{0:T(128)S(1)}, s32[64]{0:T(128)}, u32[]{:S(2)}) copy-start(s32[64]{0:T(128)} %copy-done.9) | copy-start | bytes 772
  43.1 9.8 %copy-start.3 = (bf16[32,2,64]{2,1,0:T(2,128)(2,1)S(1)}, bf16[32,2,64]{2,1,0:T(2,128)(2,1)}, u32[]{:S(2)}) copy-start(bf16[32,2,64]{2,1,0:T(2,128)(2,1)} %copy-done.2) | copy-start | bytes 24580
  48.1 11.7 %all-to-all-start.1 = ((bf16[8,32,258]{2,1,0:T(8,128)(2,1)}), bf16[8,32,258]{2,1,0:T(8,128)(2,1)S(1)}, u32[]{:S(2)}, u32[]{:S(2)}) async-start(bf16[8,32,258]{2,1,0:T(8,128)(2,1)} %bitcast.6), calls=%async_computation.1 | async-start | bytes 393216 | tf_op jit(solution)/shard_map/all_to_all | solution.py:37
  60.3 67.5 %copy-start.11 = (f32[288]{0:T(512)S(1)}, f32[288]{0:T(512)}, u32[]{:S(2)}) copy-start(f32[288]{0:T(512)} %param.18) | copy-start | bytes 3460
  109.1 18.7 %all-to-all-start.3 = ((f32[16,1,32]{2,1,0:T(1,128)}), f32[16,1,32]{2,1,0:T(1,128)S(1)}, u32[]{:S(2)}, u32[]{:S(2)}) async-start(f32[16,1,32]{2,1,0:T(1,128)} %broadcast_in_dim.64), calls=%async_computation.3 | async-start | bytes 16384 | tf_op jit(solution)/shard_map/all_to_all | solution.py:16
where the time goes:
time: 130 us; the launch traced here: 129 us
  blocking collectives  46.7 us (36%)
  matrix products  21.1 us (16%)
  waiting for transfers between devices  18 us (14%)
  starting transfers between devices  16 us (12%)
  local copies, waits for them, and re-layouts  15.9 us (12%)
  other arithmetic  10.5 us (8%)
    all_to_all x1, blocking collectives, sent_and_summed(): tiles = lax.all_to_all(in_blocks(x, dim, size), axis, 0, 0, tiled=True)  46.7 us
    all_to_all x2, waiting for transfers between devices, from_everyone(): lax.all_to_all(jnp.broadcast_to(x[None], (size, *x.shape)), axis, 0, 0, t...  11.5 us
    all_to_all x2, starting transfers between devices, from_everyone(): lax.all_to_all(jnp.broadcast_to(x[None], (size, *x.shape)), axis, 0, 0, t...  11.1 us
    gather x1, local copies, waits for them, and re-layouts, body(): task_rows = prompt_cache[jnp.clip(local_task, 0, tasks_dev - 1)]  8.41 us
    dot_general x2, matrix products, attend(): jnp.einsum('nkgd,ntkd->nkgt', query_block, block_keys, preferred_element_...  7.49 us
    all_to_all x1, waiting for transfers between devices, sent_and_summed(): tiles = lax.all_to_all(in_blocks(x, dim, size), axis, 0, 0, tiled=True)  6.53 us
    dot_general x2, matrix products, attend(): jnp.einsum('nkgt,ntkd->nkgd', weight.astype(jnp.bfloat16), block_values,...  5.68 us
    all_to_all x1, starting transfers between devices, sent_and_summed(): tiles = lax.all_to_all(in_blocks(x, dim, size), axis, 0, 0, tiled=True)  4.87 us
  transfers between devices with their start and end apart: 3, of which 2 were waited for; matrix products, arithmetic and copies ran while one was open for 16% of the time, Pallas kernels for 0%

commit v1 on v0

v1 whole, which is shorter than its diff:
```python
import functools
import math

import jax
import jax.numpy as jnp
import numpy as np
from jax import lax
from jax.experimental import pallas as pl
from jax.experimental.pallas import tpu as pltpu
from jax.sharding import PartitionSpec as P

D = 4608
H = 32
HD = 128
CAP = 50.0
EPS = 1e-6
MESH = pl.DeviceIdType.MESH
F32 = jnp.float32
BF16 = jnp.bfloat16
NT = (((1,), (1,)), ((), ()))
NN = (((1,), (0,)), ((), ()))

INNER = float(D // H) ** (-0.5) / CAP
OUTER = CAP * math.log2(math.e)


def dot(a, b, dims=NN):
    return lax.dot_general(a, b, dims, preferred_element_type=F32)


def weigh(raw):
    return jnp.exp2(OUTER * jnp.tanh(raw * INNER))


def iota(shape, dim):
    return lax.broadcasted_iota(jnp.int32, shape, dim)


def farthest_first(size):
    return sorted(range(1, size), key=lambda d: -min(d, size - d))


def layer(
    hidden_hbm,
    gain_hbm,
    wq_hbm,
    wk_hbm,
    wv_hbm,
    wo_hbm,
    post_hbm,
    pool_hbm,
    prompt_hbm,
    task_hbm,
    length_hbm,
    table_hbm,
    freq_hbm,
    out_ref,
    fresh_ref,
    hidden_v,
    gain_v,
    wq_v,
    wk_v,
    wv_v,
    wo_v,
    post_v,
    pool_v,
    prompt_v,
    task_v,
    length_v,
    table_v,
    freq_v,
    page_mix,
    all_query,
    mix_send,
    mix_recv,
    proj_send,
    proj_recv,
    square,
    in_sem,
    w_sem,
    q_send_sem,
    q_recv_sem,
    m_send_sem,
    m_recv_sem,
    p_send_sem,
    p_recv_sem,
    s_send_sem,
    s_recv_sem,
    *,
    seq,
    tensor,
    pieces,
):
    me = lax.axis_index("seq")
    mine = lax.axis_index("tensor")
    rows, width = hidden_v.shape
    requests = task_v.shape[1]
    pages = pool_v.shape[0]
    block = pool_v.shape[2]
    tasks, _, prompt, _ = prompt_v.shape
    blocks = table_v.shape[1]
    cols = out_ref.shape[1]

    seq_peer = lambda d: lax.rem(me + d, seq)
    seq_from = lambda d: lax.rem(me + seq - d, seq)
    tensor_peer = lambda d: lax.rem(mine + d, tensor)

    barrier = pltpu.get_barrier_semaphore()
    for d in range(1, seq):
        pl.semaphore_signal(barrier, inc=1, device_id={"seq": seq_peer(d)}, device_id_type=MESH)
    for d in range(1, tensor):
        pl.semaphore_signal(
            barrier, inc=1, device_id={"tensor": tensor_peer(d)}, device_id_type=MESH
        )

    small = [
        pltpu.make_async_copy(src, dst, in_sem.at[i])
        for i, (src, dst) in enumerate(
            (
                (hidden_hbm, hidden_v),
                (gain_hbm, gain_v),
                (length_hbm, length_v),
                (freq_hbm, freq_v),
                (table_hbm, table_v),
                (task_hbm, task_v),
                (post_hbm, post_v),
            )
        )
    ]
    for copy in small:
        copy.start()
    depth = width // pieces
    weights = []
    for i in range(pieces):
        part = pl.ds(i * depth, depth)
        weights.append(
            [
                pltpu.make_async_copy(src.at[part], dst.at[part], w_sem.at[3 * i + j])
                for j, (src, dst) in enumerate(
                    ((wq_hbm, wq_v), (wk_hbm, wk_v), (wv_hbm, wv_v))
                )
            ]
        )
    for group in weights:
        for copy in group:
            copy.start()
    bulk = [
        pltpu.make_async_copy(src, dst, in_sem.at[len(small) + i])
        for i, (src, dst) in enumerate(
            ((pool_hbm, pool_v), (prompt_hbm, prompt_v), (wo_hbm, wo_v))
        )
    ]
    for copy in small[:4]:
        copy.wait()

    values = hidden_v[...].astype(F32)
    scale = lax.rsqrt(jnp.mean(values * values, axis=-1, keepdims=True) + EPS)
    normed = (values * scale * gain_v[...]).astype(BF16)

    length_row = length_v[...].astype(F32)
    at = iota((rows, requests), 0) + me * rows
    own_length = jnp.sum(
        jnp.where(at == iota((rows, requests), 1), length_row, 0.0), axis=1, keepdims=True
    )
    angles = (own_length + float(prompt)) * freq_v[...]
    cosine = jnp.cos(angles)
    sine = jnp.sin(angles)
    half = HD // 2
    sine = jnp.where(iota(sine.shape, 1) < half, -sine, sine)

    heads = wq_v.shape[1] // HD
    query = jnp.zeros((rows, wq_v.shape[1]), F32)
    key = jnp.zeros((rows, HD), F32)
    value = jnp.zeros((rows, HD), F32)
    for i in range(pieces):
        for copy in weights[i]:
            copy.wait()
        if i == pieces - 1:
            for copy in bulk:
                copy.start()
        part = slice(i * depth, (i + 1) * depth)
        left = normed[:, part]
        query = query + dot(left, wq_v[part])
        key = key + dot(left, wk_v[part])
        value = value + dot(left, wv_v[part])

    def rope(x):
        return (x * cosine + pltpu.roll(x, half, 1) * sine).astype(BF16)

    own_query = [rope(query[:, h * HD : (h + 1) * HD]) for h in range(heads)]
    new_key = rope(key)
    new_value = value.astype(BF16)
    all_query[me] = jnp.concatenate(own_query, axis=1)

    pl.semaphore_wait(barrier, seq + tensor - 2)
    q_copies = []
    for d in farthest_first(seq):
        copy = pltpu.make_async_remote_copy(
            src_ref=all_query.at[me],
            dst_ref=all_query.at[me],
            send_sem=q_send_sem.at[d],
            recv_sem=q_recv_sem.at[d],
            device_id={"seq": seq_peer(d)},
            device_id_type=MESH,
        )
        copy.start()
        q_copies.append((d, copy))

    fresh_ref[:, 0, :] = new_key
    fresh_ref[:, 1, :] = new_value

    key32 = new_key.astype(F32)
    value32 = new_value.astype(F32)
    self_weight = [
        weigh(jnp.sum(q.astype(F32) * key32, axis=1, keepdims=True)) for q in own_query
    ]
    self_mix = [w.astype(BF16).astype(F32) * value32 for w in self_weight]

    small[4].wait()
    small[5].wait()
    turned = table_v[...].astype(F32).T
    page_id = (iota((pages, requests), 0) + me * pages).astype(F32)
    live = jnp.zeros((pages, requests), F32)
    for j in range(blocks):
        live = jnp.where(turned[j : j + 1, :] == page_id, length_row - float(j * block), live)
    owner = jnp.where(live > 0.0, 1.0, 0.0)
    valid = jnp.minimum(jnp.sum(live, axis=1, keepdims=True), float(block))
    owner_t = owner.T.astype(BF16)
    owner = owner.astype(BF16)

    same = iota((requests, requests), 0) == iota((requests, requests), 1)
    task = jnp.sum(
        jnp.where(same, task_v[...].astype(F32), 0.0), axis=1, keepdims=True
    ).astype(jnp.int32) - me * tasks

    for d, copy in q_copies:
        pltpu.make_async_remote_copy(
            src_ref=all_query.at[seq_from(d)],
            dst_ref=all_query.at[seq_from(d)],
            send_sem=q_send_sem.at[d],
            recv_sem=q_recv_sem.at[d],
            device_id={"seq": seq_from(d)},
            device_id_type=MESH,
        ).wait_recv()
    queries = all_query[...].reshape(requests, heads * HD)

    page_query = dot(owner, queries)
    bulk[0].wait()
    group = 8
    span = group * block
    lane = iota((heads * group, span), 1)
    row = lax.rem(iota((heads * group, span), 0), group)
    own_page = lax.div(lane, block) == row
    token = lax.rem(lane, block).astype(F32)
    token = jnp.where(own_page, token, float(2 * block))
    for g in range(pages // group):
        part = slice(g * group, (g + 1) * group)
        left = jnp.concatenate(
            [page_query[part, h * HD : (h + 1) * HD] for h in range(heads)], axis=0
        ).astype(BF16)
        count = jnp.concatenate([valid[part]] * heads, axis=0)
        raw = dot(left, pool_v[part, 0].reshape(span, HD), NT)
        weight = jnp.where(token < count, weigh(raw), 0.0)
        total = jnp.sum(weight, axis=1, keepdims=True)
        mix = dot(weight.astype(BF16), pool_v[part, 1].reshape(span, HD))
        for h in range(heads):
            page_mix[part, h * HD : (h + 1) * HD] = mix[h * group : (h + 1) * group]
        first = iota((group, HD), 1) < HD // heads
        page_mix[part, heads * HD :] = jnp.where(first, total[:group], total[group:])
    spread = dot(owner_t, page_mix[...].astype(BF16))

    bulk[1].wait()
    chunk = 8
    keys = chunk * prompt
    lane_task = lax.div(iota((requests, keys), 1), prompt)
    totals = []
    for h in range(heads):
        left = queries[:, h * HD : (h + 1) * HD]
        total = jnp.zeros((requests, 1), F32)
        mix = spread[:, h * HD : (h + 1) * HD]
        for b in range(tasks // chunk):
            part = slice(b * chunk, (b + 1) * chunk)
            raw = dot(left, prompt_v[part, 0].reshape(keys, HD), NT)
            weight = jnp.where(lane_task == task - b * chunk, weigh(raw), 0.0)
            total = total + jnp.sum(weight, axis=1, keepdims=True)
            mix = mix + dot(weight.astype(BF16), prompt_v[part, 1].reshape(keys, HD))
        mix_send[:, :, h * HD : (h + 1) * HD] = mix.astype(BF16).reshape(seq, rows, HD)
        totals.append(total)
    first = iota((requests, HD), 1) < HD // heads
    mix_send[:, :, heads * HD :] = (
        (spread[:, heads * HD :] + jnp.where(first, totals[0], totals[1]))
        .astype(BF16)
        .reshape(seq, rows, HD)
    )

    m_copies = []
    for d in farthest_first(seq):
        copy = pltpu.make_async_remote_copy(
            src_ref=mix_send.at[seq_peer(d)],
            dst_ref=mix_recv.at[d],
            send_sem=m_send_sem.at[d],
            recv_sem=m_recv_sem.at[d],
            device_id={"seq": seq_peer(d)},
            device_id_type=MESH,
        )
        copy.start()
        m_copies.append(copy)
    whole = mix_send[me].astype(F32)
    bulk[2].wait()
    small[6].wait()
    for copy in m_copies:
        copy.wait_recv()
    for d in range(1, seq):
        whole = whole + mix_recv[d].astype(F32)
    attended = []
    for h in range(heads):
        at = heads * HD + h * (HD // heads)
        total = whole[:, at : at + 1] + self_weight[h]
        mix = whole[:, h * HD : (h + 1) * HD] + self_mix[h]
        attended.append((mix / total).astype(BF16))
    projected = dot(jnp.concatenate(attended, axis=1), wo_v[...])

    tail = cols % HD
    full = cols // HD
    fold = HD // tail
    step = rows // fold
    for k in range(tensor):
        piece = projected[:, k * cols : (k + 1) * cols]
        for f in range(full):
            proj_send[k, f * rows : (f + 1) * rows] = piece[:, f * HD : (f + 1) * HD].astype(BF16)
        end = piece[:, full * HD :]
        proj_send[k, full * rows :] = jnp.concatenate(
            [end[i * step : (i + 1) * step] for i in range(fold)], axis=1
        ).astype(BF16)
    p_copies = []
    for d in farthest_first(tensor):
        copy = pltpu.make_async_remote_copy(
            src_ref=proj_send.at[tensor_peer(d)],
            dst_ref=proj_recv.at[d],
            send_sem=p_send_sem.at[d],
            recv_sem=p_recv_sem.at[d],
            device_id={"tensor": tensor_peer(d)},
            device_id_type=MESH,
        )
        copy.start()
        p_copies.append(copy)
    share = proj_send[mine].astype(F32)
    start = mine * cols
    base = lax.div(start, HD) * HD
    reach = (full + 1) * HD
    residual = hidden_v[:, pl.ds(pl.multiple_of(base, HD), reach)].astype(F32)
    residual = pltpu.roll(residual, lax.rem(reach - (start - base), reach), 1)
    for copy in p_copies:
        copy.wait_recv()
    for d in range(1, tensor):
        share = share + proj_recv[d].astype(F32)

    squares = share * share
    body_sum = squares[:rows]
    for f in range(1, full):
        body_sum = body_sum + squares[f * rows : (f + 1) * rows]
    body_sum = jnp.sum(body_sum, axis=1, keepdims=True)
    ends = squares[full * rows :]
    lane = iota((step, HD), 1)
    down = iota((step, HD), 0)
    line = jnp.zeros((step, HD), F32)
    for i in range(fold):
        of_end = jnp.sum(
            jnp.where(lax.div(lane, tail) == i, ends, 0.0), axis=1, keepdims=True
        )
        line = jnp.where(
            lane == i * tail + down, body_sum[i * step : (i + 1) * step] + of_end, line
        )
    square[0] = jnp.sum(line, axis=0, keepdims=True)
    s_copies = []
    for d in farthest_first(tensor):
        copy = pltpu.make_async_remote_copy(
            src_ref=square.at[0],
            dst_ref=square.at[d],
            send_sem=s_send_sem.at[d],
            recv_sem=s_recv_sem.at[d],
            device_id={"tensor": tensor_peer(d)},
            device_id_type=MESH,
        )
        copy.start()
        s_copies.append(copy)
    for copy in s_copies:
        copy.wait_recv()
    summed = square[0]
    for d in range(1, tensor):
        summed = summed + square[d]
    inverse = lax.rsqrt(summed * (1.0 / width) + EPS)
    columns = [
        jnp.sum(jnp.where(lane == i * tail + down, inverse, 0.0), axis=1, keepdims=True)
        for i in range(fold)
    ]
    post = post_v[...]
    inverse = jnp.concatenate(columns, axis=0)
    for f in range(full):
        part = slice(f * HD, (f + 1) * HD)
        out_ref[:, part] = (
            residual[:, part] + share[f * rows : (f + 1) * rows] * inverse * post[:, part]
        ).astype(BF16)
    end = jnp.concatenate(
        [share[full * rows :, i * tail : (i + 1) * tail] for i in range(fold)], axis=0
    )
    out_ref[:, full * HD :] = (
        residual[:, full * HD : cols] + end * inverse * post[:, full * HD :]
    ).astype(BF16)

    for _, copy in q_copies:
        copy.wait_send()
    for copy in m_copies + p_copies + s_copies:
        copy.wait_send()


def body(
    seq,
    tensor,
    hidden,
    pre_gain,
    w_query,
    w_key,
    w_value,
    w_out,
    post_gain,
    cache_pool,
    prompt_cache,
    task_ids,
    cache_lengths,
    block_table,
):
    rows, width = hidden.shape
    cols = post_gain.shape[0]
    heads = w_query.shape[1] // HD
    pages = cache_pool.shape[0]
    lines = rows * cols // HD
    pieces = 6
    half = HD // 2
    freq = np.float32(10000.0) ** (-np.arange(half, dtype=np.float64) / half)
    freq = jnp.asarray(np.concatenate([freq, freq])[None].astype(np.float32))
    args = (
        hidden,
        pre_gain.reshape(1, -1),
        w_query,
        w_key,
        w_value,
        w_out,
        post_gain.reshape(1, -1),
        cache_pool,
        prompt_cache,
        task_ids.reshape(1, -1),
        cache_lengths.reshape(1, -1),
        block_table,
        freq,
    )
    wide = (heads + 1) * HD
    dma = pltpu.SemaphoreType.DMA
    return pl.pallas_call(
        functools.partial(layer, seq=seq, tensor=tensor, pieces=pieces),
        out_shape=(
            jax.ShapeDtypeStruct((rows, cols), BF16),
            jax.ShapeDtypeStruct((rows, 2, HD), BF16),
        ),
        in_specs=[pl.BlockSpec(memory_space=pltpu.HBM)] * len(args),
        out_specs=[pl.BlockSpec(memory_space=pltpu.VMEM)] * 2,
        scratch_shapes=[pltpu.VMEM(a.shape, a.dtype) for a in args]
        + [
            pltpu.VMEM((pages, wide), F32),
            pltpu.VMEM((seq, rows, heads * HD), BF16),
            pltpu.VMEM((seq, rows, wide), BF16),
            pltpu.VMEM((seq, rows, wide), BF16),
            pltpu.VMEM((tensor, lines, HD), BF16),
            pltpu.VMEM((tensor, lines, HD), BF16),
            pltpu.VMEM((tensor, 1, HD), F32),
            dma((10,)),
            dma((3 * pieces,)),
            dma((seq,)),
            dma((seq,)),
            dma((seq,)),
            dma((seq,)),
            dma((tensor,)),
            dma((tensor,)),
            dma((tensor,)),
            dma((tensor,)),
        ],
        compiler_params=pltpu.CompilerParams(
            collective_id=0, has_side_effects=True, vmem_limit_bytes=60 * 1024 * 1024
        ),
        name="layer",
    )(*args)


def solution(mesh):
    seq = mesh.shape["seq"]
    tensor = mesh.shape["tensor"]
    return jax.shard_map(
        functools.partial(body, seq, tensor),
        mesh=mesh,
        in_specs=(
            P(("groups", "seq"), None),
            P(),
            P(None, "tensor"),
            P(None, "tensor"),
            P(None, "tensor"),
            P("tensor", None),
            P("tensor"),
            P(("groups", "seq"), None, None, "tensor"),
            P("seq", None, None, "tensor"),
            P("groups"),
            P("groups"),
            P("groups", None),
        ),
        out_specs=(P(("groups", "seq"), "tensor"), P(("groups", "seq"), None, "tensor")),
        check_vma=False,
    )
```

time: 130 us -> 72.7 us (0.56)
  Pallas kernels: 0 us -> 64.8 us
  blocking collectives: 46.7 us -> 0 us
  matrix products: 21.1 us -> 0 us
  waiting for transfers between devices: 18 us -> 0 us
  starting transfers between devices: 16 us -> 0 us
  other arithmetic: 10.5 us -> 0 us
  local copies, waits for them, and re-layouts: 15.9 us -> 6.78 us
    pallas_call x0 -> x1, Pallas kernels: none -> 64.8 us  [body(): pl.pallas_call(functools.partial(layer, seq=seq, tensor=tensor, pieces=pi...]
    all_to_all x1 -> x0, blocking collectives: 46.7 us -> none  [sent_and_summed(): tiles = lax.all_to_all(in_blocks(x, dim, size), axis, 0, 0, tiled=True)]
    dot_general x11 -> x0, matrix products: 21.1 us -> none  [the longest x2 7.49 us: attend(): jnp.einsum('nkgd,ntkd->nkgt', query_block, block_keys, preferred_element_...]
    all_to_all x3 -> x0, waiting for transfers between devices: 18 us -> none  [the longest x2 11.5 us: from_everyone(): lax.all_to_all(jnp.broadcast_to(x[None], (size, *x.shape)), axis, 0, 0, t...]
    all_to_all x3 -> x0, starting transfers between devices: 16 us -> none  [the longest x2 11.1 us: from_everyone(): lax.all_to_all(jnp.broadcast_to(x[None], (size, *x.shape)), axis, 0, 0, t...]
    gather x1 -> x0, local copies, waits for them, and re-layouts: 8.41 us -> none  [body(): task_rows = prompt_cache[jnp.clip(local_task, 0, tasks_dev - 1)]]
    reduce_sum x8 -> x0, other arithmetic: 3.69 us -> none  [the longest x1 1.28 us: rms_scale(): mean_square = jnp.mean(values * values, axis=-1, keepdims=True)]
    reshape x3 -> x2, local copies, waits for them, and re-layouts: 0.67 us -> 2.59 us  [the longest x1 1.35 us: body(): pre_gain.reshape(1, -1)]
  transfers between devices with their start and end apart: 3 -> 0, of which waited for: 2 -> 0; matrix products, arithmetic and copies ran while one was open for 16% -> 0% of each run, Pallas kernels for 0% -> 0%
where the time goes in v1:
time: 72.7 us; the launch traced here: 72.2 us
  Pallas kernels  64.8 us (89%)
  local copies, waits for them, and re-layouts  6.78 us (9%)
    pallas_call x1, Pallas kernels, body(): pl.pallas_call(functools.partial(layer, seq=seq, tensor=tensor, pieces=pi...  64.8 us
    unnamed x3, local copies, waits for them, and re-layouts  4.19 us

profile of v1, /device:TPU:40, one launch (start us, length us, event | category | flops | bytes accessed | tf_op | source)
XLA Modules:
  0.0 72.2 jit_solution(13231643699840816132)
XLA Ops:
  0.6 1.2 %reshape.17.post_hbm = f32[1,288]{1,0:T(1,128)} reshape(f32[288]{0:T(512)} %param.19) | data formatting | bytes 2304 | tf_op jit(solution)/shard_map/reshape | solution.py:449
  1.9 1.3 %reshape.16.gain_hbm = f32[1,4608]{1,0:T(1,128)} reshape(f32[4608]{0:T(1024)} %param.14) | data formatting | bytes 36864 | tf_op jit(solution)/shard_map/reshape | solution.py:444
  3.2 1.5 %copy.15.table_hbm = s32[256,32]{1,0:T(8,128)} copy(s32[256,32]{0,1:T(8,128)} %param.24) | data formatting | bytes 65536 | tf_op args[11]
  4.7 64.8 %layer.1 = (bf16[32,288]{1,0:T(8,128)(2,1)}, bf16[32,2,128]{2,1,0:T(2,128)(2,1)}) custom-call(bf16[32,4608]{1,0:T(8,128)(2,1)} %hidden_hbm.1, f32[1,4608]{1,0:T(1,128)} %reshape.16.gain_hbm, bf16[4608,256]{1,0:T(8,128)(2,1)} %wq_hbm.1, bf16[4608,128]{1,0:T(8,128)(2,1)} %wk_hbm.1, bf16[4608,128]{1,0:T(8,128)(2,1)} %wv_hbm.1, bf16[256,4608]{1,0:T(8,128)(2,1)} %wo_hbm.1, ...), custom_call_target="tpu_custom_call" | custom-call | tf_op jit(solution)/shard_map/layer/pallas_call | solution.py:459
  69.5 1.3 %copy.18 = bf16[32,288]{1,0:T(8,128)(2,1)} copy(bf16[32,288]{1,0:T(8,128)(2,1)} %get-tuple-element.4) | data formatting | bytes 36864
  70.9 1.3 %copy.19 = bf16[32,2,128]{2,1,0:T(2,128)(2,1)} copy(bf16[32,2,128]{2,1,0:T(2,128)(2,1)} %get-tuple-element.5) | data formatting | bytes 32768

commit v2 on v1

--- a/solution.py
+++ b/solution.py
@@ -34,6 +34,14 @@
 
 def iota(shape, dim):
     return lax.broadcasted_iota(jnp.int32, shape, dim)
+
+
+def spread_lanes(columns, lane):
+    width = lane.shape[1] // len(columns)
+    out = jnp.broadcast_to(columns[0], lane.shape)
+    for i in range(1, len(columns)):
+        out = jnp.where(lane >= i * width, columns[i], out)
+    return out
 
 
 def farthest_first(size):
@@ -70,12 +78,16 @@
     table_v,
     freq_v,
     page_mix,
+    prompt_mix,
+    prompt_total,
+    task_column,
     all_query,
     mix_send,
     mix_recv,
     proj_send,
     proj_recv,
     square,
+    here,
     in_sem,
     w_sem,
     q_send_sem,
@@ -98,20 +110,34 @@
     pages = pool_v.shape[0]
     block = pool_v.shape[2]
     tasks, _, prompt, _ = prompt_v.shape
-    blocks = table_v.shape[1]
+    blocks = table_v.shape[0]
     cols = out_ref.shape[1]
 
-    seq_peer = lambda d: lax.rem(me + d, seq)
-    seq_from = lambda d: lax.rem(me + seq - d, seq)
+    chips = seq // 2
+    chip, core = lax.div(me, 2), lax.rem(me, 2)
+    slot = lambda ahead, other: lax.rem(chip + ahead, chips) * 2 + lax.rem(core + other, 2)
+    source = lambda ahead, other: slot((chips - ahead) % chips, other)
+    routes = [
+        (ahead, other)
+        for ahead in farthest_first(chips) + [0]
+        for other in (1, 0)
+        if ahead + other > 0
+    ]
     tensor_peer = lambda d: lax.rem(mine + d, tensor)
 
+    at_place = lambda p: (p + 1) % tensor
+    place = lax.rem(mine + tensor - 1, tensor)
+
     barrier = pltpu.get_barrier_semaphore()
-    for d in range(1, seq):
-        pl.semaphore_signal(barrier, inc=1, device_id={"seq": seq_peer(d)}, device_id_type=MESH)
-    for d in range(1, tensor):
-        pl.semaphore_signal(
-            barrier, inc=1, device_id={"tensor": tensor_peer(d)}, device_id_type=MESH
-        )
+    for route in routes:
+        pl.semaphore_signal(barrier, inc=1, device_id={"seq": slot(*route)}, device_id_type=MESH)
+    for p in range(1, tensor):
+
+        @pl.when(place < p)
+        def _(p=p):
+            pl.semaphore_signal(
+                barrier, inc=1, device_id={"tensor": at_place(p)}, device_id_type=MESH
+            )
 
     small = [
         pltpu.make_async_copy(src, dst, in_sem.at[i])
@@ -141,7 +167,7 @@
                 )
             ]
         )
-    for group in weights:
+    for group in weights[: pieces // 2]:
         for copy in group:
             copy.start()
     bulk = [
@@ -150,12 +176,16 @@
             ((pool_hbm, pool_v), (prompt_hbm, prompt_v), (wo_hbm, wo_v))
         )
     ]
+
     for copy in small[:4]:
         copy.wait()
+    for group in weights[pieces // 2 :]:
+        for copy in group:
+            copy.start()
 
     values = hidden_v[...].astype(F32)
     scale = lax.rsqrt(jnp.mean(values * values, axis=-1, keepdims=True) + EPS)
-    normed = (values * scale * gain_v[...]).astype(BF16)
+    normed = (values * scale * gain_v[...].reshape(1, -1)).astype(BF16)
 
     length_row = length_v[...].astype(F32)
     at = iota((rows, requests), 0) + me * rows
@@ -192,19 +222,26 @@
     new_value = value.astype(BF16)
     all_query[me] = jnp.concatenate(own_query, axis=1)
 
-    pl.semaphore_wait(barrier, seq + tensor - 2)
-    q_copies = []
-    for d in farthest_first(seq):
-        copy = pltpu.make_async_remote_copy(
+    pl.semaphore_wait(barrier, seq - 1 + place)
+    for p in range(tensor - 1):
+
+        @pl.when(p < place)
+        def _(p=p):
+            pl.semaphore_signal(
+                here.at[place], inc=1, device_id={"tensor": at_place(p)}, device_id_type=MESH
+            )
+
+    q_copies = {}
+    for ahead, other in routes:
+        q_copies[ahead, other] = pltpu.make_async_remote_copy(
             src_ref=all_query.at[me],
             dst_ref=all_query.at[me],
-            send_sem=q_send_sem.at[d],
-            recv_sem=q_recv_sem.at[d],
-            device_id={"seq": seq_peer(d)},
+            send_sem=q_send_sem.at[2 * ahead + other],
+            recv_sem=q_recv_sem.at[2 * ahead + other],
+            device_id={"seq": slot(ahead, other)},
             device_id_type=MESH,
         )
-        copy.start()
-        q_copies.append((d, copy))
+        q_copies[ahead, other].start()
 
     fresh_ref[:, 0, :] = new_key
     fresh_ref[:, 1, :] = new_value
@@ -216,9 +253,55 @@
     ]
     self_mix = [w.astype(BF16).astype(F32) * value32 for w in self_weight]
 
+    small[5].wait()
+    same = iota((requests, requests), 0) == iota((requests, requests), 1)
+    task = jnp.sum(
+        jnp.where(same, task_v[...].astype(F32), 0.0), axis=1, keepdims=True
+    ).astype(jnp.int32) - me * tasks
+    task_column[...] = jnp.broadcast_to(task, (requests, HD)).reshape(seq, rows, HD)
+
+    chunk = 8
+    keys = chunk * prompt
+
+    def attend_prompts(slots):
+        left = jnp.concatenate(
+            [all_query[s, :, h * HD : (h + 1) * HD] for s in slots for h in range(heads)], axis=0
+        )
+        wanted = jnp.concatenate(
+            [task_column[s, :, :1] for s in slots for h in range(heads)], axis=0
+        )
+        count = left.shape[0]
+        lane_task = lax.div(iota((count, keys), 1), prompt)
+        total = jnp.zeros((count, 1), F32)
+        mix = jnp.zeros((count, HD), F32)
+        for b in range(tasks // chunk):
+            part = slice(b * chunk, (b + 1) * chunk)
+            raw = dot(left, prompt_v[part, 0].reshape(keys, HD), NT)
+            weight = jnp.where(lane_task == wanted - b * chunk, weigh(raw), 0.0)
+            total = total + jnp.sum(weight, axis=1, keepdims=True)
+            mix = mix + dot(weight.astype(BF16), prompt_v[part, 1].reshape(keys, HD))
+        span = heads * rows
+        for i, s in enumerate(slots):
+            prompt_mix[s] = mix[i * span : (i + 1) * span]
+            prompt_total[s] = jnp.broadcast_to(total[i * span : (i + 1) * span], (span, HD))
+
+    def arrive(route):
+        came = source(*route)
+        pltpu.make_async_remote_copy(
+            src_ref=all_query.at[came],
+            dst_ref=all_query.at[came],
+            send_sem=q_send_sem.at[2 * route[0] + route[1]],
+            recv_sem=q_recv_sem.at[2 * route[0] + route[1]],
+            device_id={"seq": came},
+            device_id_type=MESH,
+        ).wait_recv()
+        return came
+
+    bulk[1].wait()
+    attend_prompts([me])
+
     small[4].wait()
-    small[5].wait()
-    turned = table_v[...].astype(F32).T
+    turned = table_v[...].astype(F32)
     page_id = (iota((pages, requests), 0) + me * pages).astype(F32)
     live = jnp.zeros((pages, requests), F32)
     for j in range(blocks):
@@ -228,20 +311,13 @@
     owner_t = owner.T.astype(BF16)
     owner = owner.astype(BF16)
 
-    same = iota((requests, requests), 0) == iota((requests, requests), 1)
-    task = jnp.sum(
-        jnp.where(same, task_v[...].astype(F32), 0.0), axis=1, keepdims=True
-    ).astype(jnp.int32) - me * tasks
-
-    for d, copy in q_copies:
-        pltpu.make_async_remote_copy(
-            src_ref=all_query.at[seq_from(d)],
-            dst_ref=all_query.at[seq_from(d)],
-            send_sem=q_send_sem.at[d],
-            recv_sem=q_recv_sem.at[d],
-            device_id={"seq": seq_from(d)},
-            device_id_type=MESH,
-        ).wait_recv()
+    far = farthest_first(chips)
+    arrivals = [[(0, 1)], [(a, o) for a in far if a in (1, chips - 1) for o in (0, 1)]]
+    rest = [(a, o) for a in far if a not in (1, chips - 1) for o in (0, 1)]
+    if rest:
+        arrivals.append(rest)
+    for batch in arrivals:
+        attend_prompts([arrive(route) for route in batch])
     queries = all_query[...].reshape(requests, heads * HD)
 
     page_query = dot(owner, queries)
@@ -265,42 +341,44 @@
         mix = dot(weight.astype(BF16), pool_v[part, 1].reshape(span, HD))
         for h in range(heads):
             page_mix[part, h * HD : (h + 1) * HD] = mix[h * group : (h + 1) * group]
-        first = iota((group, HD), 1) < HD // heads
-        page_mix[part, heads * HD :] = jnp.where(first, total[:group], total[group:])
+        high = total.astype(BF16).astype(F32)
+        low = total - high
+        fine = iota((group, HD), 1)
+        columns = [x[h * group : (h + 1) * group] for h in range(heads) for x in (high, low)]
+        page_mix[part, heads * HD :] = spread_lanes(columns, fine)
     spread = dot(owner_t, page_mix[...].astype(BF16))
 
-    bulk[1].wait()
-    chunk = 8
-    keys = chunk * prompt
-    lane_task = lax.div(iota((requests, keys), 1), prompt)
-    totals = []
+    lanes = HD // (2 * heads)
+    sums = []
     for h in range(heads):
-        left = queries[:, h * HD : (h + 1) * HD]
-        total = jnp.zeros((requests, 1), F32)
-        mix = spread[:, h * HD : (h + 1) * HD]
-        for b in range(tasks // chunk):
-            part = slice(b * chunk, (b + 1) * chunk)
-            raw = dot(left, prompt_v[part, 0].reshape(keys, HD), NT)
-            weight = jnp.where(lane_task == task - b * chunk, weigh(raw), 0.0)
-            total = total + jnp.sum(weight, axis=1, keepdims=True)
-            mix = mix + dot(weight.astype(BF16), prompt_v[part, 1].reshape(keys, HD))
-        mix_send[:, :, h * HD : (h + 1) * HD] = mix.astype(BF16).reshape(seq, rows, HD)
-        totals.append(total)
-    first = iota((requests, HD), 1) < HD // heads
-    mix_send[:, :, heads * HD :] = (
-        (spread[:, heads * HD :] + jnp.where(first, totals[0], totals[1]))
-        .astype(BF16)
-        .reshape(seq, rows, HD)
-    )
+        part = slice(h * rows, (h + 1) * rows)
+        mix_send[:, part] = (
+            spread[:, h * HD : (h + 1) * HD].reshape(seq, rows, HD) + prompt_mix[:, part]
+        ).astype(BF16)
+        at = heads * HD + 2 * h * lanes
+        sums.append(
+            spread[:, at : at + 1]
+            + spread[:, at + lanes : at + lanes + 1]
+            + prompt_total[:, part, :1].reshape(requests, 1)
+        )
+    fine = iota((8, HD), 1)
+    for j in range(seq):
+        columns = []
+        for h in range(heads):
+            for q in range(rows // 8):
+                total = sums[h][j * rows + q * 8 : j * rows + q * 8 + 8]
+                high = total.astype(BF16).astype(F32)
+                columns += [high, total - high]
+        mix_send[j, heads * rows :] = spread_lanes(columns, fine).astype(BF16)
 
     m_copies = []
-    for d in farthest_first(seq):
+    for ahead, other in routes:
         copy = pltpu.make_async_remote_copy(
-            src_ref=mix_send.at[seq_peer(d)],
-            dst_ref=mix_recv.at[d],
-            send_sem=m_send_sem.at[d],
-            recv_sem=m_recv_sem.at[d],
-            device_id={"seq": seq_peer(d)},
+            src_ref=mix_send.at[slot(ahead, other)],
+            dst_ref=mix_recv.at[2 * ahead + other],
+            send_sem=m_send_sem.at[2 * ahead + other],
+            recv_sem=m_recv_sem.at[2 * ahead + other],
+            device_id={"seq": slot(ahead, other)},
             device_id_type=MESH,
         )
         copy.start()
@@ -312,11 +390,21 @@
         copy.wait_recv()
     for d in range(1, seq):
         whole = whole + mix_recv[d].astype(F32)
+    table = whole[heads * rows :]
     attended = []
     for h in range(heads):
-        at = heads * HD + h * (HD // heads)
-        total = whole[:, at : at + 1] + self_weight[h]
-        mix = whole[:, h * HD : (h + 1) * HD] + self_mix[h]
+        line = rows // 8
+        lanes = HD // (2 * heads * line)
+        total = jnp.concatenate(
+            [
+                table[:, (2 * q) * lanes : (2 * q) * lanes + 1]
+                + table[:, (2 * q + 1) * lanes : (2 * q + 1) * lanes + 1]
+                for q in range(h * line, (h + 1) * line)
+            ],
+            axis=0,
+        )
+        total = total + self_weight[h]
+        mix = whole[h * rows : (h + 1) * rows] + self_mix[h]
         attended.append((mix / total).astype(BF16))
     projected = dot(jnp.concatenate(attended, axis=1), wo_v[...])
 
@@ -332,9 +420,8 @@
         proj_send[k, full * rows :] = jnp.concatenate(
             [end[i * step : (i + 1) * step] for i in range(fold)], axis=1
         ).astype(BF16)
-    p_copies = []
-    for d in farthest_first(tensor):
-        copy = pltpu.make_async_remote_copy(
+    p_copies = [
+        pltpu.make_async_remote_copy(
             src_ref=proj_send.at[tensor_peer(d)],
             dst_ref=proj_recv.at[d],
             send_sem=p_send_sem.at[d],
@@ -342,8 +429,15 @@
             device_id={"tensor": tensor_peer(d)},
             device_id_type=MESH,
         )
-        copy.start()
-        p_copies.append(copy)
+        for d in range(1, tensor)
+    ]
+    for d in farthest_first(tensor):
+
+        @pl.when(place + d < tensor)
+        def _(d=d):
+            pl.semaphore_wait(here.at[place + d], 1)
+
+        p_copies[d - 1].start()
     share = proj_send[mine].astype(F32)
     start = mine * cols
     base = lax.div(start, HD) * HD
@@ -394,7 +488,7 @@
         jnp.sum(jnp.where(lane == i * tail + down, inverse, 0.0), axis=1, keepdims=True)
         for i in range(fold)
     ]
-    post = post_v[...]
+    post = post_v[...].reshape(1, -1)
     inverse = jnp.concatenate(columns, axis=0)
     for f in range(full):
         part = slice(f * HD, (f + 1) * HD)
@@ -408,10 +502,15 @@
         residual[:, full * HD : cols] + end * inverse * post[:, full * HD :]
     ).astype(BF16)
 
-    for _, copy in q_copies:
+    for copy in q_copies.values():
         copy.wait_send()
     for copy in m_copies + p_copies + s_copies:
         copy.wait_send()
+
+
+def hand_out(out_ref, fresh_ref, out, fresh):
+    out[...] = out_ref[...]
+    fresh[...] = fresh_ref[...]
 
 
 def body(
@@ -441,38 +540,42 @@
     freq = jnp.asarray(np.concatenate([freq, freq])[None].astype(np.float32))
     args = (
         hidden,
-        pre_gain.reshape(1, -1),
+        pre_gain,
         w_query,
         w_key,
         w_value,
         w_out,
-        post_gain.reshape(1, -1),
+        post_gain,
         cache_pool,
         prompt_cache,
         task_ids.reshape(1, -1),
         cache_lengths.reshape(1, -1),
-        block_table,
+        block_table.T,
         freq,
     )
     wide = (heads + 1) * HD
     dma = pltpu.SemaphoreType.DMA
-    return pl.pallas_call(
+    outs = pl.pallas_call(
         functools.partial(layer, seq=seq, tensor=tensor, pieces=pieces),
         out_shape=(
-            jax.ShapeDtypeStruct((rows, cols), BF16),
-            jax.ShapeDtypeStruct((rows, 2, HD), BF16),
+            pltpu.VMEM((rows, cols), BF16),
+            pltpu.VMEM((rows, 2, HD), BF16),
         ),
         in_specs=[pl.BlockSpec(memory_space=pltpu.HBM)] * len(args),
         out_specs=[pl.BlockSpec(memory_space=pltpu.VMEM)] * 2,
         scratch_shapes=[pltpu.VMEM(a.shape, a.dtype) for a in args]
         + [
             pltpu.VMEM((pages, wide), F32),
+            pltpu.VMEM((seq, heads * rows, HD), F32),
+            pltpu.VMEM((seq, heads * rows, HD), F32),
+            pltpu.VMEM((seq, rows, HD), jnp.int32),
             pltpu.VMEM((seq, rows, heads * HD), BF16),
-            pltpu.VMEM((seq, rows, wide), BF16),
-            pltpu.VMEM((seq, rows, wide), BF16),
+            pltpu.VMEM((seq, heads * rows + 8, HD), BF16),
+            pltpu.VMEM((seq, heads * rows + 8, HD), BF16),
             pltpu.VMEM((tensor, lines, HD), BF16),
             pltpu.VMEM((tensor, lines, HD), BF16),
             pltpu.VMEM((tensor, 1, HD), F32),
+            pltpu.SemaphoreType.REGULAR((tensor,)),
             dma((10,)),
             dma((3 * pieces,)),
             dma((seq,)),
@@ -489,6 +592,13 @@
         ),
         name="layer",
     )(*args)
+    return pl.pallas_call(
+        hand_out,
+        out_shape=tuple(jax.ShapeDtypeStruct(a.shape, a.dtype) for a in outs),
+        in_specs=[pl.BlockSpec(memory_space=pltpu.VMEM)] * 2,
+        out_specs=[pl.BlockSpec(memory_space=pltpu.VMEM)] * 2,
+        name="hand_out",
+    )(*(pltpu.with_memory_space_constraint(a, pltpu.VMEM) for a in outs))
 
 
 def solution(mesh):

time: 72.7 us -> 59.8 us (0.82)
  local copies, waits for them, and re-layouts: 6.78 us -> 0 us
  Pallas kernels: 64.8 us -> 59 us
    pallas_call x1, Pallas kernels: 64.8 us -> 58.4 us  [body(): pl.pallas_call(functools.partial(layer, seq=seq, tensor=tensor, pieces=pi...]
    unnamed x3 -> x0, local copies, waits for them, and re-layouts: 4.19 us -> none
    reshape x2 -> x0, local copies, waits for them, and re-layouts: 2.59 us -> none  [the longest x1 1.35 us: body(): pre_gain.reshape(1, -1)]
where the time goes in v2:
time: 59.8 us; the launch traced here: 59.6 us
  Pallas kernels  59 us (99%)
  between operations  0.64 us (1%)
    pallas_call x1, Pallas kernels, body(): pl.pallas_call(functools.partial(layer, seq=seq, tensor=tensor, pieces=pi...  58.4 us

profile of v2, /device:TPU:40, one launch (start us, length us, event | category | flops | bytes accessed | tf_op | source)
XLA Modules:
  0.0 59.6 jit_solution(10235629225456125416)
XLA Ops:
  0.6 58.4 %layer.1 = (bf16[32,288]{1,0:T(8,128)(2,1)S(1)}, bf16[32,2,128]{2,1,0:T(2,128)(2,1)S(1)}) custom-call(bf16[32,4608]{1,0:T(8,128)(2,1)} %hidden_hbm.1, f32[4608]{0:T(1024)} %gain_hbm.1, bf16[4608,256]{1,0:T(8,128)(2,1)} %wq_hbm.1, bf16[4608,128]{1,0:T(8,128)(2,1)} %wk_hbm.1, bf16[4608,128]{1,0:T(8,128)(2,1)} %wv_hbm.1, bf16[256,4608]{1,0:T(8,128)(2,1)} %wo_hbm.1, ...), custom_call_target="tpu_custom_call" | custom-call | tf_op jit(solution)/shard_map/layer/pallas_call | solution.py:558
  59.0 0.6 %hand_out.1 = (bf16[32,288]{1,0:T(8,128)(2,1)}, bf16[32,2,128]{2,1,0:T(2,128)(2,1)}) custom-call(bf16[32,288]{1,0:T(8,128)(2,1)S(1)} %get-tuple-element.4.out_ref, bf16[32,2,128]{2,1,0:T(2,128)(2,1)S(1)} %get-tuple-element.5.fresh_ref), custom_call_target="tpu_custom_call" | custom-call | tf_op jit(solution)/shard_map/hand_out/pallas_call | solution.py:595

commit v3 on v2

--- a/solution.py
+++ b/solution.py
@@ -139,6 +139,9 @@
                 barrier, inc=1, device_id={"tensor": at_place(p)}, device_id_type=MESH
             )
 
+    def arrived(ref, sem):
+        pltpu.make_async_copy(ref, ref, sem).wait()
+
     small = [
         pltpu.make_async_copy(src, dst, in_sem.at[i])
         for i, (src, dst) in enumerate(
@@ -161,10 +164,8 @@
         part = pl.ds(i * depth, depth)
         weights.append(
             [
-                pltpu.make_async_copy(src.at[part], dst.at[part], w_sem.at[3 * i + j])
-                for j, (src, dst) in enumerate(
-                    ((wq_hbm, wq_v), (wk_hbm, wk_v), (wv_hbm, wv_v))
-                )
+                pltpu.make_async_copy(src.at[part], dst.at[part], w_sem.at[i])
+                for src, dst in ((wq_hbm, wq_v), (wk_hbm, wk_v), (wv_hbm, wv_v))
             ]
         )
     for group in weights[: pieces // 2]:
@@ -203,11 +204,12 @@
     key = jnp.zeros((rows, HD), F32)
     value = jnp.zeros((rows, HD), F32)
     for i in range(pieces):
-        for copy in weights[i]:
-            copy.wait()
+        arrived(wq_v.at[pl.ds(0, 2 * depth)], w_sem.at[i])
+        if i == pieces // 2:
+            bulk[1].start()
         if i == pieces - 1:
-            for copy in bulk:
-                copy.start()
+            bulk[0].start()
+            bulk[2].start()
         part = slice(i * depth, (i + 1) * depth)
         left = normed[:, part]
         query = query + dot(left, wq_v[part])
@@ -236,7 +238,7 @@
         q_copies[ahead, other] = pltpu.make_async_remote_copy(
             src_ref=all_query.at[me],
             dst_ref=all_query.at[me],
-            send_sem=q_send_sem.at[2 * ahead + other],
+            send_sem=q_send_sem,
             recv_sem=q_recv_sem.at[2 * ahead + other],
             device_id={"seq": slot(ahead, other)},
             device_id_type=MESH,
@@ -290,7 +292,7 @@
         pltpu.make_async_remote_copy(
             src_ref=all_query.at[came],
             dst_ref=all_query.at[came],
-            send_sem=q_send_sem.at[2 * route[0] + route[1]],
+            send_sem=q_send_sem,
             recv_sem=q_recv_sem.at[2 * route[0] + route[1]],
             device_id={"seq": came},
             device_id_type=MESH,
@@ -371,23 +373,20 @@
                 columns += [high, total - high]
         mix_send[j, heads * rows :] = spread_lanes(columns, fine).astype(BF16)
 
-    m_copies = []
     for ahead, other in routes:
         copy = pltpu.make_async_remote_copy(
             src_ref=mix_send.at[slot(ahead, other)],
             dst_ref=mix_recv.at[2 * ahead + other],
-            send_sem=m_send_sem.at[2 * ahead + other],
-            recv_sem=m_recv_sem.at[2 * ahead + other],
+            send_sem=m_send_sem,
+            recv_sem=m_recv_sem,
             device_id={"seq": slot(ahead, other)},
             device_id_type=MESH,
         )
         copy.start()
-        m_copies.append(copy)
     whole = mix_send[me].astype(F32)
     bulk[2].wait()
     small[6].wait()
-    for copy in m_copies:
-        copy.wait_recv()
+    arrived(mix_recv.at[pl.ds(1, seq - 1)], m_recv_sem)
     for d in range(1, seq):
         whole = whole + mix_recv[d].astype(F32)
     table = whole[heads * rows :]
@@ -420,32 +419,27 @@
         proj_send[k, full * rows :] = jnp.concatenate(
             [end[i * step : (i + 1) * step] for i in range(fold)], axis=1
         ).astype(BF16)
-    p_copies = [
+    for d in farthest_first(tensor):
+
+        @pl.when(place + d < tensor)
+        def _(d=d):
+            pl.semaphore_wait(here.at[place + d], 1)
+
         pltpu.make_async_remote_copy(
             src_ref=proj_send.at[tensor_peer(d)],
             dst_ref=proj_recv.at[d],
-            send_sem=p_send_sem.at[d],
-            recv_sem=p_recv_sem.at[d],
+            send_sem=p_send_sem,
+            recv_sem=p_recv_sem,
             device_id={"tensor": tensor_peer(d)},
             device_id_type=MESH,
-        )
-        for d in range(1, tensor)
-    ]
-    for d in farthest_first(tensor):
-
-        @pl.when(place + d < tensor)
-        def _(d=d):
-            pl.semaphore_wait(here.at[place + d], 1)
-
-        p_copies[d - 1].start()
+        ).start()
     share = proj_send[mine].astype(F32)
     start = mine * cols
     base = lax.div(start, HD) * HD
     reach = (full + 1) * HD
     residual = hidden_v[:, pl.ds(pl.multiple_of(base, HD), reach)].astype(F32)
     residual = pltpu.roll(residual, lax.rem(reach - (start - base), reach), 1)
-    for copy in p_copies:
-        copy.wait_recv()
+    arrived(proj_recv.at[pl.ds(1, tensor - 1)], p_recv_sem)
     for d in range(1, tensor):
         share = share + proj_recv[d].astype(F32)
 
@@ -466,20 +460,17 @@
             lane == i * tail + down, body_sum[i * step : (i + 1) * step] + of_end, line
         )
     square[0] = jnp.sum(line, axis=0, keepdims=True)
-    s_copies = []
     for d in farthest_first(tensor):
         copy = pltpu.make_async_remote_copy(
             src_ref=square.at[0],
             dst_ref=square.at[d],
-            send_sem=s_send_sem.at[d],
-            recv_sem=s_recv_sem.at[d],
+            send_sem=s_send_sem,
+            recv_sem=s_recv_sem,
             device_id={"tensor": tensor_peer(d)},
             device_id_type=MESH,
         )
         copy.start()
-        s_copies.append(copy)
-    for copy in s_copies:
-        copy.wait_recv()
+    arrived(square.at[pl.ds(1, tensor - 1)], s_recv_sem)
     summed = square[0]
     for d in range(1, tensor):
         summed = summed + square[d]
@@ -502,10 +493,10 @@
         residual[:, full * HD : cols] + end * inverse * post[:, full * HD :]
     ).astype(BF16)
 
-    for copy in q_copies.values():
-        copy.wait_send()
-    for copy in m_copies + p_copies + s_copies:
-        copy.wait_send()
+    arrived(all_query.at[pl.ds(0, seq - 1)], q_send_sem)
+    arrived(mix_send.at[pl.ds(0, seq - 1)], m_send_sem)
+    arrived(proj_send.at[pl.ds(0, tensor - 1)], p_send_sem)
+    arrived(square.at[pl.ds(0, tensor - 1)], s_send_sem)
 
 
 def hand_out(out_ref, fresh_ref, out, fresh):
@@ -577,16 +568,11 @@
             pltpu.VMEM((tensor, 1, HD), F32),
             pltpu.SemaphoreType.REGULAR((tensor,)),
             dma((10,)),
-            dma((3 * pieces,)),
+            dma((pieces,)),
+            dma,
             dma((seq,)),
-            dma((seq,)),
-            dma((seq,)),
-            dma((seq,)),
-            dma((tensor,)),
-            dma((tensor,)),
-            dma((tensor,)),
-            dma((tensor,)),
-        ],
+        ]
+        + [dma] * 6,
         compiler_params=pltpu.CompilerParams(
             collective_id=0, has_side_effects=True, vmem_limit_bytes=60 * 1024 * 1024
         ),

time: 59.8 us -> 58.3 us (0.975)
  Pallas kernels: 59 us -> 57.5 us
    pallas_call x1, Pallas kernels: 58.4 us -> 56.9 us  [body(): pl.pallas_call(functools.partial(layer, seq=seq, tensor=tensor, pieces=pi...]
where the time goes in v3:
time: 58.3 us; the launch traced here: 58.2 us
  Pallas kernels  57.5 us (99%)
  between operations  0.64 us (1%)
    pallas_call x1, Pallas kernels, body(): pl.pallas_call(functools.partial(layer, seq=seq, tensor=tensor, pieces=pi...  56.9 us

profile of v3, /device:TPU:40, one launch (start us, length us, event | category | flops | bytes accessed | tf_op | source)
XLA Modules:
  0.0 58.2 jit_solution(3651153709368721476)
XLA Ops:
  0.6 56.9 %layer.1 = (bf16[32,288]{1,0:T(8,128)(2,1)S(1)}, bf16[32,2,128]{2,1,0:T(2,128)(2,1)S(1)}) custom-call(bf16[32,4608]{1,0:T(8,128)(2,1)} %hidden_hbm.1, f32[4608]{0:T(1024)} %gain_hbm.1, bf16[4608,256]{1,0:T(8,128)(2,1)} %wq_hbm.1, bf16[4608,128]{1,0:T(8,128)(2,1)} %wk_hbm.1, bf16[4608,128]{1,0:T(8,128)(2,1)} %wv_hbm.1, bf16[256,4608]{1,0:T(8,128)(2,1)} %wo_hbm.1, ...), custom_call_target="tpu_custom_call" | custom-call | tf_op jit(solution)/shard_map/layer/pallas_call | solution.py:549
  57.6 0.6 %hand_out.1 = (bf16[32,288]{1,0:T(8,128)(2,1)}, bf16[32,2,128]{2,1,0:T(2,128)(2,1)}) custom-call(bf16[32,288]{1,0:T(8,128)(2,1)S(1)} %get-tuple-element.4.out_ref, bf16[32,2,128]{2,1,0:T(2,128)(2,1)S(1)} %get-tuple-element.5.fresh_ref), custom_call_target="tpu_custom_call" | custom-call | tf_op jit(solution)/shard_map/hand_out/pallas_call | solution.py:581

commit v4 on v3

--- a/solution.py
+++ b/solution.py
@@ -128,17 +128,6 @@
     at_place = lambda p: (p + 1) % tensor
     place = lax.rem(mine + tensor - 1, tensor)
 
-    barrier = pltpu.get_barrier_semaphore()
-    for route in routes:
-        pl.semaphore_signal(barrier, inc=1, device_id={"seq": slot(*route)}, device_id_type=MESH)
-    for p in range(1, tensor):
-
-        @pl.when(place < p)
-        def _(p=p):
-            pl.semaphore_signal(
-                barrier, inc=1, device_id={"tensor": at_place(p)}, device_id_type=MESH
-            )
-
     def arrived(ref, sem):
         pltpu.make_async_copy(ref, ref, sem).wait()
 
@@ -178,6 +167,17 @@
         )
     ]
 
+    barrier = pltpu.get_barrier_semaphore()
+    for route in routes:
+        pl.semaphore_signal(barrier, inc=1, device_id={"seq": slot(*route)}, device_id_type=MESH)
+    for p in range(1, tensor):
+
+        @pl.when(place < p)
+        def _(p=p):
+            pl.semaphore_signal(
+                barrier, inc=1, device_id={"tensor": at_place(p)}, device_id_type=MESH
+            )
+
     for copy in small[:4]:
         copy.wait()
     for group in weights[pieces // 2 :]:
@@ -198,6 +198,24 @@
     sine = jnp.sin(angles)
     half = HD // 2
     sine = jnp.where(iota(sine.shape, 1) < half, -sine, sine)
+
+    small[5].wait()
+    same = iota((requests, requests), 0) == iota((requests, requests), 1)
+    task = jnp.sum(
+        jnp.where(same, task_v[...].astype(F32), 0.0), axis=1, keepdims=True
+    ).astype(jnp.int32) - me * tasks
+    task_column[...] = jnp.broadcast_to(task, (requests, HD)).reshape(seq, rows, HD)
+
+    small[4].wait()
+    turned = table_v[...].astype(F32)
+    page_id = (iota((pages, requests), 0) + me * pages).astype(F32)
+    live = jnp.zeros((pages, requests), F32)
+    for j in range(blocks):
+        live = jnp.where(turned[j : j + 1, :] == page_id, length_row - float(j * block), live)
+    owner = jnp.where(live > 0.0, 1.0, 0.0)
+    valid = jnp.minimum(jnp.sum(live, axis=1, keepdims=True), float(block))
+    owner_t = owner.T.astype(BF16)
+    owner = owner.astype(BF16)
 
     heads = wq_v.shape[1] // HD
     query = jnp.zeros((rows, wq_v.shape[1]), F32)
@@ -225,14 +243,6 @@
     all_query[me] = jnp.concatenate(own_query, axis=1)
 
     pl.semaphore_wait(barrier, seq - 1 + place)
-    for p in range(tensor - 1):
-
-        @pl.when(p < place)
-        def _(p=p):
-            pl.semaphore_signal(
-                here.at[place], inc=1, device_id={"tensor": at_place(p)}, device_id_type=MESH
-            )
-
     q_copies = {}
     for ahead, other in routes:
         q_copies[ahead, other] = pltpu.make_async_remote_copy(
@@ -245,6 +255,14 @@
         )
         q_copies[ahead, other].start()
 
+    for p in range(tensor - 1):
+
+        @pl.when(p < place)
+        def _(p=p):
+            pl.semaphore_signal(
+                here.at[place], inc=1, device_id={"tensor": at_place(p)}, device_id_type=MESH
+            )
+
     fresh_ref[:, 0, :] = new_key
     fresh_ref[:, 1, :] = new_value
 
@@ -254,13 +272,6 @@
         weigh(jnp.sum(q.astype(F32) * key32, axis=1, keepdims=True)) for q in own_query
     ]
     self_mix = [w.astype(BF16).astype(F32) * value32 for w in self_weight]
-
-    small[5].wait()
-    same = iota((requests, requests), 0) == iota((requests, requests), 1)
-    task = jnp.sum(
-        jnp.where(same, task_v[...].astype(F32), 0.0), axis=1, keepdims=True
-    ).astype(jnp.int32) - me * tasks
-    task_column[...] = jnp.broadcast_to(task, (requests, HD)).reshape(seq, rows, HD)
 
     chunk = 8
     keys = chunk * prompt
@@ -301,17 +312,6 @@
 
     bulk[1].wait()
     attend_prompts([me])
-
-    small[4].wait()
-    turned = table_v[...].astype(F32)
-    page_id = (iota((pages, requests), 0) + me * pages).astype(F32)
-    live = jnp.zeros((pages, requests), F32)
-    for j in range(blocks):
-        live = jnp.where(turned[j : j + 1, :] == page_id, length_row - float(j * block), live)
-    owner = jnp.where(live > 0.0, 1.0, 0.0)
-    valid = jnp.minimum(jnp.sum(live, axis=1, keepdims=True), float(block))
-    owner_t = owner.T.astype(BF16)
-    owner = owner.astype(BF16)
 
     far = farthest_first(chips)
     arrivals = [[(0, 1)], [(a, o) for a in far if a in (1, chips - 1) for o in (0, 1)]]

time: 58.3 us -> 57.5 us (0.986)
  Pallas kernels: 57.5 us -> 56.7 us
    pallas_call x1, Pallas kernels: 56.9 us -> 56.1 us  [body(): pl.pallas_call(functools.partial(layer, seq=seq, tensor=tensor, pieces=pi...]
where the time goes in v4:
time: 57.5 us; the launch traced here: 57.3 us
  Pallas kernels  56.7 us (99%)
  between operations  0.64 us (1%)
    pallas_call x1, Pallas kernels, body(): pl.pallas_call(functools.partial(layer, seq=seq, tensor=tensor, pieces=pi...  56.1 us

profile of v4, /device:TPU:40, one launch (start us, length us, event | category | flops | bytes accessed | tf_op | source)
XLA Modules:
  0.0 57.3 jit_solution(16571147850291719683)
XLA Ops:
  0.6 56.1 %layer.1 = (bf16[32,288]{1,0:T(8,128)(2,1)S(1)}, bf16[32,2,128]{2,1,0:T(2,128)(2,1)S(1)}) custom-call(bf16[32,4608]{1,0:T(8,128)(2,1)} %hidden_hbm.1, f32[4608]{0:T(1024)} %gain_hbm.1, bf16[4608,256]{1,0:T(8,128)(2,1)} %wq_hbm.1, bf16[4608,128]{1,0:T(8,128)(2,1)} %wk_hbm.1, bf16[4608,128]{1,0:T(8,128)(2,1)} %wv_hbm.1, bf16[256,4608]{1,0:T(8,128)(2,1)} %wo_hbm.1, ...), custom_call_target="tpu_custom_call" | custom-call | tf_op jit(solution)/shard_map/layer/pallas_call | solution.py:549
  56.7 0.6 %hand_out.1 = (bf16[32,288]{1,0:T(8,128)(2,1)}, bf16[32,2,128]{2,1,0:T(2,128)(2,1)}) custom-call(bf16[32,288]{1,0:T(8,128)(2,1)S(1)} %get-tuple-element.4.out_ref, bf16[32,2,128]{2,1,0:T(2,128)(2,1)S(1)} %get-tuple-element.5.fresh_ref), custom_call_target="tpu_custom_call" | custom-call | tf_op jit(solution)/shard_map/hand_out/pallas_call | solution.py:581

commit v5 on v4

--- a/solution.py
+++ b/solution.py
@@ -273,8 +273,6 @@
     ]
     self_mix = [w.astype(BF16).astype(F32) * value32 for w in self_weight]
 
-    chunk = 8
-    keys = chunk * prompt
 
     def attend_prompts(slots):
         left = jnp.concatenate(
@@ -284,6 +282,8 @@
             [task_column[s, :, :1] for s in slots for h in range(heads)], axis=0
         )
         count = left.shape[0]
+        chunk = tasks
+        keys = chunk * prompt
         lane_task = lax.div(iota((count, keys), 1), prompt)
         total = jnp.zeros((count, 1), F32)
         mix = jnp.zeros((count, HD), F32)

time: 57.5 us -> 57 us (level)
  no operation moved by 1% of the time
where the time goes in v5:
time: 57 us; the launch traced here: 56.9 us
  Pallas kernels  56.2 us (99%)
  between operations  0.64 us (1%)
    pallas_call x1, Pallas kernels, body(): pl.pallas_call(functools.partial(layer, seq=seq, tensor=tensor, pieces=pi...  55.6 us

profile of v5, /device:TPU:40, one launch (start us, length us, event | category | flops | bytes accessed | tf_op | source)
XLA Modules:
  0.0 56.9 jit_solution(15101013442603412394)
XLA Ops:
  0.6 55.6 %layer.1 = (bf16[32,288]{1,0:T(8,128)(2,1)S(1)}, bf16[32,2,128]{2,1,0:T(2,128)(2,1)S(1)}) custom-call(bf16[32,4608]{1,0:T(8,128)(2,1)} %hidden_hbm.1, f32[4608]{0:T(1024)} %gain_hbm.1, bf16[4608,256]{1,0:T(8,128)(2,1)} %wq_hbm.1, bf16[4608,128]{1,0:T(8,128)(2,1)} %wk_hbm.1, bf16[4608,128]{1,0:T(8,128)(2,1)} %wv_hbm.1, bf16[256,4608]{1,0:T(8,128)(2,1)} %wo_hbm.1, ...), custom_call_target="tpu_custom_call" | custom-call | tf_op jit(solution)/shard_map/layer/pallas_call | solution.py:549
  56.2 0.6 %hand_out.1 = (bf16[32,288]{1,0:T(8,128)(2,1)}, bf16[32,2,128]{2,1,0:T(2,128)(2,1)}) custom-call(bf16[32,288]{1,0:T(8,128)(2,1)S(1)} %get-tuple-element.4.out_ref, bf16[32,2,128]{2,1,0:T(2,128)(2,1)S(1)} %get-tuple-element.5.fresh_ref), custom_call_target="tpu_custom_call" | custom-call | tf_op jit(solution)/shard_map/hand_out/pallas_call | solution.py:581
